TPU v7x, 32 devices: a whole 2x2x4 slice. The times are simulated.
32 devices in a mesh: seq: 8 (over y, x, core), adapter: 4 (over z).
Axes of the slice: x: 2, y: 2, z: 4, core: 2. Of those that a mesh axis runs over, the one named last changes fastest.
Arguments:
- hidden: bfloat16 [8, 1024, 8192], P('adapter', 'seq'), may hold values from -6 to 6
- response_base_queries: bfloat16 [8, 1024, 1024], P('adapter', 'seq'), may hold values from -6 to 6
- attention_output_gradient: bfloat16 [8, 1024, 1024], P('adapter', 'seq'), may hold values from -6 to 6
- keys: bfloat16 [6144, 128], P('seq'), may hold values from -6 to 6
- values: bfloat16 [6144, 128], P('seq'), may hold values from -6 to 6
- adapter_down_weight: bfloat16 [8, 16, 8192], P('adapter'), may hold values from -0.0625 to 0.0625
- adapter_up_weight: bfloat16 [8, 16, 1024], P('adapter'), may hold values from -1.5 to 1.5
- lengths: int32 [8], P('adapter'), may hold values from 512 to 1024
- offsets: int32 [8, 1024], P('adapter', 'seq'), may hold values from 0 to 6143, as said below
Outputs:
- adapter_down_gradient: float32 [8, 16, 8192], P('adapter', None, 'seq')
- adapter_up_gradient: float32 [8, 16, 1024], P('adapter')
- prompt_key_gradient: float32 [6144, 128], P(('seq', 'adapter'))
- prompt_value_gradient: float32 [6144, 128], P(('seq', 'adapter'))
Inputs may be any that keep to these rules, and one draw needn't show every extreme that they name: Row r of every adapter has offsets in [(r // 128) * 768, (r // 128 + 1) * 768).
All inputs are finite; a program needn't handle non-finite values.
Results may differ from a plain program's by a relative error of at most 0.025.
The roundings to bfloat16 on the way count: a program that leaves them out, or rounds other values in their place, can miss the bound.
Values may be sent and summed in bfloat16 or wider, within the bound.
A program may use at most 192 MiB of HBM per device.

v0:
```python
import functools

import jax
import jax.numpy as jnp
from jax import lax
from jax.experimental import pallas as pl
from jax.experimental.pallas import tpu as pltpu
from jax.sharding import PartitionSpec as P

adapter_scale = 2.0
masked_score = -1e30
MESH = pl.DeviceIdType.MESH
VMEM = pltpu.VMEM


def to_seq(index):
    return dict(device_id={"seq": index}, device_id_type=MESH)


def to_adapter(index):
    return dict(device_id={"adapter": index}, device_id_type=MESH)


def remote(src, dst, send_sem, recv_sem, target):
    return pltpu.make_async_remote_copy(
        src_ref=src, dst_ref=dst, send_sem=send_sem, recv_sem=recv_sem, **target
    )


def dot(a, b, dims):
    return lax.dot_general(a, b, (dims, ((), ())), preferred_element_type=jnp.float32)


def attend_kernel(
    n, nz, heads, chunk,
    len_ref, hidden_hbm, base_hbm, grad_hbm, down_w, up_w, offset_ref, keys_ref, values_ref,
    down_out, up_out, prompt_out,
    low_ref, dq_ref, part, hidden, base, grad, q_all, g_all, k_all, v_all, kt, s_ref, p_ref, peaks, place_ref,
    key_acc, value_acc, prob_all, ds_all, load_sem, send_sem, recv_sem,
    down, up, pair_a, pair_b, back_two, back_three, summed, total, z_in, down_in, up_in, up_mine,
    pair_send, pair_recv, back_send, back_recv, z_send, z_recv, d_send, d_recv, u_send, u_recv,
    ag_send, ag_recv,
):
    s = lax.axis_index("seq")
    core = s % 2
    partner = s + 1 - 2 * core
    adapt_n, rows, _ = base.shape
    stretch, hd = keys_ref.shape
    tiles, wide, _ = q_all.shape
    per = tiles // adapt_n
    factor = hd**-0.5
    pieces = stretch // chunk
    loads = [
        pltpu.make_async_copy(a, b, load_sem.at[i])
        for i, (a, b) in enumerate(((hidden_hbm, hidden), (base_hbm, base), (grad_hbm, grad)))
    ]
    for c in loads:
        c.start()
    full = (k_all, v_all)
    own = (keys_ref, values_ref)

    def copy(i, src, slot, which, target):
        return remote(src, full[i].at[slot], send_sem.at[which, i], recv_sem.at[slot, i], to_seq(target))

    two_on = [copy(i, own[i], 2, 0, s + 2) for i in range(2)]
    three_on = [copy(i, own[i], 3, 1, s + 3) for i in range(2)]
    next_on = [copy(i, own[i], 1, 1, s + 1) for i in range(2)]
    hand_up = [copy(i, full[i].at[2], 3, 2, s + 1) for i in range(2)]
    hand_down = [copy(i, full[i].at[2], 1, 2, s - 1) for i in range(2)]

    def arrived(slot, i):
        @pl.when(s >= slot)
        def _():
            remote(
                full[i].at[slot], full[i].at[slot], send_sem.at[0, i], recv_sem.at[slot, i], to_seq(partner)
            ).wait_recv()

    z = lax.axis_index("adapter")
    has_three_in = (core == 1) & (s + 3 < n)

    @pl.when(s + 2 >= n)
    def _():
        back_two[...] = jnp.zeros_like(back_two)

    @pl.when(jnp.logical_not(has_three_in))
    def _():
        back_three[...] = jnp.zeros_like(back_three)

    @pl.when(core == 1)
    def _():
        pair_b[...] = jnp.zeros_like(pair_b)

    barrier = pltpu.get_barrier_semaphore()
    for i in range(1, n):
        pl.semaphore_signal(barrier, inc=1, **to_seq((s + i) % n))
    for i in range(1, nz):
        pl.semaphore_signal(barrier, inc=1, **to_adapter((z + i) % nz))
    pl.semaphore_wait(barrier, n - 1 + nz - 1)

    has_two_on = s + 2 < n
    has_three_on = (core == 1) & (s + 3 < n)
    for i in range(2):

        @pl.when(has_two_on)
        def _():
            two_on[i].start()

        @pl.when(has_three_on)
        def _():
            three_on[i].start()

        @pl.when(core == 0)
        def _():
            next_on[i].start()

    k_all[0] = keys_ref[...]
    v_all[0] = values_ref[...]
    for slot in (1, 2, 3):

        @pl.when(s < slot)
        def _():
            k_all[slot] = jnp.zeros(k_all.shape[1:], k_all.dtype)
            v_all[slot] = jnp.zeros(v_all.shape[1:], v_all.dtype)

    key_acc[...] = jnp.zeros_like(key_acc)
    value_acc[...] = jnp.zeros_like(value_acc)
    for c in loads:
        c.wait()
    for a in range(adapt_n):
        low = dot(hidden[a], down_w[a], ((1,), (1,))).astype(jnp.bfloat16)
        low_ref[a] = low
        place = jnp.concatenate([offset_ref[a]] * heads, axis=1) - s * stretch
        for t in range(per):
            place_ref[a * per + t] = place
        raised = dot(low, up_w[a], ((1,), (0,)))
        query = (base[a].astype(jnp.float32) + adapter_scale * raised).astype(jnp.bfloat16)
        live = s * rows + lax.broadcasted_iota(jnp.int32, (rows, 1), 0) < len_ref[a]
        g = jnp.where(live, grad[a], jnp.zeros_like(grad[a]))
        for h in range(per * heads):
            t, at_row = a * per + h // heads, (h % heads) * rows
            q_all[t, at_row : at_row + rows, :] = query[:, h * hd : (h + 1) * hd]
            g_all[t, at_row : at_row + rows, :] = g[:, h * hd : (h + 1) * hd]

    def hand(i):
        @pl.when(s >= 2)
        def _():
            @pl.when(core == 0)
            def _():
                hand_up[i].start()

            @pl.when(core == 1)
            def _():
                hand_down[i].start()

    def at(piece):
        return slice(piece * chunk, (piece + 1) * chunk)

    def before(piece, place):
        pos = piece * chunk + lax.broadcasted_iota(jnp.int32, (chunk, wide), 0)
        return pos <= place

    def turned(d):
        kt[:, d * stretch : (d + 1) * stretch] = k_all[d].T

    peaks[...] = jnp.full(peaks.shape, masked_score, jnp.float32)

    def scores_of(d):
        bias = jnp.where(s >= d, 0.0, masked_score)

        @pl.loop(0, tiles)
        def _(t):
            q = q_all[t]
            peak = peaks[t]
            for piece in range(pieces):
                score = dot(k_all[d, at(piece), :], q, ((1,), (1,))) * factor + bias
                s_ref[t, at(d * pieces + piece), :] = score
                peak = jnp.maximum(peak, jnp.max(score, axis=0, keepdims=True))
            peaks[t] = peak

    arrived(2, 0)
    hand(0)
    turned(2)
    scores_of(2)
    arrived(1, 0)
    turned(1)
    scores_of(1)
    arrived(2, 1)
    hand(1)
    arrived(3, 0)
    turned(3)
    turned(0)
    far = jnp.where(s >= 3, 1.0, 0.0)
    far_bias = jnp.where(s >= 3, 0.0, masked_score)

    @pl.loop(0, tiles)
    def _(t):
        q = q_all[t]
        peak = peaks[t]
        place = place_ref[t]
        for piece in range(pieces):
            near = dot(k_all[0, at(piece), :], q, ((1,), (1,))) * factor
            other = dot(k_all[3, at(piece), :], q, ((1,), (1,))) * (factor * far) + far_bias
            score = jnp.where(before(piece, place), near, other)
            s_ref[t, at(piece), :] = score
            peak = jnp.maximum(peak, jnp.max(score, axis=0, keepdims=True))
        peaks[t] = peak

    arrived(1, 1)
    arrived(3, 1)
    units = [(0, piece) for piece in range(pieces)]
    units += [(d, piece) for d in (1, 2) for piece in range(pieces)]

    @pl.loop(0, tiles)
    def _(t):
        q = q_all[t]
        g = g_all[t]
        peak = peaks[t]
        place = place_ref[t]
        total = jnp.zeros((1, wide), jnp.float32)
        inner = jnp.zeros((1, wide), jnp.float32)
        for u, (d, piece) in enumerate(units):
            e = jnp.exp(s_ref[t, at(u), :] - peak)
            dp = dot(v_all[d, at(piece), :], g, ((1,), (1,)))
            if d == 0:
                other = dot(v_all[3, at(piece), :], g, ((1,), (1,)))
                dp = jnp.where(before(piece, place), dp, other)
            s_ref[t, at(u), :] = e
            p_ref[at(u), :] = dp
            total = total + jnp.sum(e, axis=0, keepdims=True)
            inner = inner + jnp.sum(e * dp, axis=0, keepdims=True)
        inverse = 1.0 / total
        delta = inner * inverse
        dq = jnp.zeros((hd, wide), jnp.float32)
        for u, (d, piece) in enumerate(units):
            prob = s_ref[t, at(u), :] * inverse
            ds = prob * (p_ref[at(u), :] - delta)
            if d == 0:
                near = before(piece, place)
                cases = [
                    (0, jnp.where(near, prob, 0.0), jnp.where(near, ds, 0.0)),
                    (3, jnp.where(near, 0.0, prob), jnp.where(near, 0.0, ds)),
                ]
            else:
                cases = [(d, prob, ds)]
            for block, prob_part, ds_part in cases:
                prob_low = prob_part.astype(jnp.bfloat16)
                ds_low = ds_part.astype(jnp.bfloat16)
                if d == 0:
                    value_acc[block // 3, at(piece), :] += dot(prob_low, g, ((1,), (0,)))
                    key_acc[block // 3, at(piece), :] += dot(ds_low, q, ((1,), (0,)))
                else:
                    columns = pl.ds(pl.multiple_of(t * wide, 128), wide)
                    prob_all[at(u - pieces), columns] = prob_low
                    ds_all[at(u - pieces), columns] = ds_low
                begin = block * stretch + piece * chunk
                dq = dq + dot(kt[:, begin : begin + chunk], ds_low, ((1,), (0,)))
        dq_ref[t] = (dq * factor).T.astype(jnp.bfloat16)

    width = down_out.shape[1]
    quarter = prompt_out.shape[1]
    has_far = (core == 0) & (s >= 3)

    def pair_copy(d, to, i, j):
        return remote(part.at[d, i], to.at[i], pair_send.at[j, i], pair_recv.at[j, i], to_seq(partner))

    zero_to_one = [pair_copy(1, pair_a, i, 0) for i in range(2)]
    one_to_zero = [pair_copy(3, pair_a, i, 0) for i in range(2)]
    near_back = [pair_copy(1, pair_b, i, 1) for i in range(2)]
    far_back = [
        remote(part.at[3, i], back_three.at[i], back_send.at[1, i], back_recv.at[1, i], to_seq(s - 3))
        for i in range(2)
    ]
    two_back = [
        remote(summed.at[i], back_two.at[i], back_send.at[0, i], back_recv.at[0, i], to_seq(s - 2))
        for i in range(2)
    ]
    def summed_up(d, i):
        for piece in range(pieces):
            if d in (0, 3):
                if i == 0:
                    part[d, 0, at(piece), :] = (key_acc[d // 3, at(piece), :] * factor).astype(jnp.bfloat16)
                else:
                    part[d, 1, at(piece), :] = value_acc[d // 3, at(piece), :].astype(jnp.bfloat16)
                continue
            weights = (ds_all, prob_all)[i][at((d - 1) * pieces + piece), :]
            other = (q_all, g_all)[i][...].reshape(tiles * wide, hd)
            out = dot(weights, other, ((1,), (0,)))
            part[d, i, at(piece), :] = (out if i else out * factor).astype(jnp.bfloat16)

    downs, ups, gathers = [], [], []
    for i in range(1, n):
        peer = (s + i) % n
        columns = pl.ds(pl.multiple_of(peer * width, 128), width)
        downs.append(
            remote(down.at[:, columns], down_in.at[i - 1], d_send.at[i - 1], d_recv.at[i - 1], to_seq(peer))
        )
        ups.append(remote(up.at[peer], up_in.at[i - 1], u_send.at[i - 1], u_recv.at[i - 1], to_seq(peer)))
        gathers.append(remote(up_mine, up_out.at[s], ag_send.at[i - 1], ag_recv.at[i - 1], to_seq(peer)))

    def sum_pair(i):
        zero_to_one[i].wait_recv()
        summed[i] = (part[2, i].astype(jnp.float32) + pair_a[i].astype(jnp.float32)).astype(jnp.bfloat16)

        @pl.when(s >= 2)
        def _():
            two_back[i].start()

    for i in (1, 0):
        summed_up(3, i)

        @pl.when(core == 1)
        def _():
            one_to_zero[i].start()

        @pl.when(has_far)
        def _():
            far_back[i].start()

    for i in (1, 0):
        summed_up(1, i)

        @pl.when(core == 0)
        def _():
            zero_to_one[i].start()

        @pl.when(core == 1)
        def _():
            near_back[i].start()

        summed_up(2, i)
        sum_pair(i)
    _, rank, feature_n = up_w.shape
    group = feature_n // hd
    shards, up_rows, _ = up.shape
    for a in range(adapt_n):
        small = jnp.zeros((rows, rank), jnp.float32)
        for h in range(group):
            place = a * group + h
            dq_h = dq_ref[place // heads, (place % heads) * rows : (place % heads + 1) * rows, :]
            up_h = dot(low_ref[a], dq_h, ((0,), (0,)))
            for r in range(0, rank, min(rank, up_rows)):
                spot = (h * adapt_n + a) * rank + r
                begin = spot % up_rows
                up[spot // up_rows, begin : begin + min(rank, up_rows), :] = up_h[r : r + min(rank, up_rows)]
            small = small + dot(dq_h, up_w[a, :, h * hd : (h + 1) * hd], ((1,), (1,)))
        down[a * rank : (a + 1) * rank, :] = dot(
            small.astype(jnp.bfloat16), hidden[a], ((0,), (0,))
        ).astype(jnp.bfloat16)
    for c in ups + downs:
        c.start()
    spread = [[], []]
    summed_up(0, 1)
    summed_up(0, 0)

    def owner(i):
        @pl.when(core == 0)
        def _():
            near_back[i].wait_recv()

        @pl.when(s + 2 < n)
        def _():
            two_back[i].wait_recv()

        @pl.when(has_three_in)
        def _():
            far_back[i].wait_recv()

        total[i] = (
            part[0, i].astype(jnp.float32)
            + pair_b[i].astype(jnp.float32)
            + back_two[i].astype(jnp.float32)
            + back_three[i].astype(jnp.float32)
        ).astype(jnp.bfloat16)
        for j in range(1, nz):
            peer = (z + j) % nz
            c = remote(
                total.at[i, pl.ds(pl.multiple_of(peer * quarter, 16), quarter), :],
                z_in.at[j - 1, i], z_send.at[j - 1, i], z_recv.at[j - 1, i], to_adapter(peer),
            )
            c.start()
            spread[i].append(c)

    def prompt_sum(i):
        mine = total[i, pl.ds(pl.multiple_of(z * quarter, 16), quarter), :].astype(jnp.float32)
        for j, c in enumerate(spread[i]):
            c.wait_recv()
            mine = mine + z_in[j, i].astype(jnp.float32)
        prompt_out[i] = mine

    owner(1)
    mine = up[s]
    for i, c in enumerate(ups):
        c.wait_recv()
        mine = mine + up_in[i]
    up_mine[...] = mine
    for c in gathers:
        c.start()
    up_out[s] = mine
    owner(0)
    mine = down[:, pl.ds(pl.multiple_of(s * width, 128), width)].astype(jnp.float32)
    for i, c in enumerate(downs):
        c.wait_recv()
        mine = mine + down_in[i].astype(jnp.float32)
    down_out[...] = mine
    prompt_sum(1)
    prompt_sum(0)
    for c in gathers:
        c.wait_recv()
    for c in downs + ups + gathers + spread[0] + spread[1] + zero_to_one:
        c.wait_send()
    for i in range(2):

        @pl.when(core == 1)
        def _():
            near_back[i].wait_send()

        @pl.when(has_far)
        def _():
            far_back[i].wait_send()

        @pl.when(s >= 2)
        def _():
            two_back[i].wait_send()

    for i in range(2):

        @pl.when(has_two_on)
        def _():
            two_on[i].wait_send()

        @pl.when(has_three_on)
        def _():
            three_on[i].wait_send()

        @pl.when(core == 0)
        def _():
            next_on[i].wait_send()

        @pl.when(s >= 2)
        def _():
            hand_up[i].wait_send()


def gradients(n, nz, hidden, base, grad, down_w, up_w, lengths, offsets, keys, values):
    adapt_n, row_n, feature_n = base.shape
    stretch, hd = keys.shape
    rank, model = down_w.shape[1:]
    ranks = adapt_n * rank
    heads = 4
    wide = heads * row_n
    tiles = adapt_n * feature_n // (hd * heads)
    chunk = 256 if stretch % 256 == 0 else stretch
    quarter = stretch // nz
    up_shape = (n, ranks * feature_n // (n * hd), hd)
    spec = pl.BlockSpec(memory_space=VMEM)
    anywhere = pl.BlockSpec(memory_space=pl.ANY)
    dma = pltpu.SemaphoreType.DMA
    bf16 = jnp.bfloat16
    f32 = jnp.float32
    block = VMEM((2, stretch, hd), bf16)
    return pl.pallas_call(
        functools.partial(attend_kernel, n, nz, heads, chunk),
        out_shape=(
            jax.ShapeDtypeStruct((ranks, model // n), f32),
            jax.ShapeDtypeStruct(up_shape, f32),
            jax.ShapeDtypeStruct((2, quarter, hd), f32),
        ),
        in_specs=[pl.BlockSpec(memory_space=pltpu.SMEM)] + [anywhere] * 3 + [spec] * 5,
        out_specs=(spec, spec, spec),
        scratch_shapes=[
            VMEM((adapt_n, row_n, rank), bf16),
            VMEM((tiles, wide, hd), bf16),
            VMEM((4, 2, stretch, hd), bf16),
            VMEM(hidden.shape, bf16),
            VMEM(base.shape, bf16),
            VMEM(grad.shape, bf16),
            VMEM((tiles, wide, hd), bf16),
            VMEM((tiles, wide, hd), bf16),
            VMEM((4, stretch, hd), bf16),
            VMEM((4, stretch, hd), bf16),
            VMEM((hd, 4 * stretch), bf16),
            VMEM((tiles, 3 * stretch, wide), f32),
            VMEM((3 * stretch, wide), f32),
            VMEM((tiles, 1, wide), f32),
            VMEM((tiles, 1, wide), jnp.int32),
            VMEM((2, stretch, hd), f32),
            VMEM((2, stretch, hd), f32),
            VMEM((2 * stretch, tiles * wide), bf16),
            VMEM((2 * stretch, tiles * wide), bf16),
            dma((3,)), dma((3, 2)), dma((4, 2)),
            VMEM((ranks, model), bf16),
            VMEM(up_shape, f32),
            block, block, block, block, block, block,
            VMEM((nz - 1, 2, quarter, hd), bf16),
            VMEM((n - 1, ranks, model // n), bf16),
            VMEM((n - 1,) + up_shape[1:], f32),
            VMEM(up_shape[1:], f32),
            dma((2, 2)), dma((2, 2)), dma((2, 2)), dma((2, 2)), dma((nz - 1, 2)), dma((nz - 1, 2)),
            dma((n - 1,)), dma((n - 1,)), dma((n - 1,)), dma((n - 1,)), dma((n - 1,)), dma((n - 1,)),
        ],
        compiler_params=pltpu.CompilerParams(
            collective_id=0, has_side_effects=True, vmem_limit_bytes=60 * 1024 * 1024
        ),
        name="gradients",
    )(lengths, hidden, base, grad, down_w, up_w, offsets[:, None, :], keys, values)


def finish_kernel(down_hbm, up_hbm, prompt_hbm, down_out, up_out, key_out, value_out, down, up, sems):
    adapt_n, rank, _ = down_out.shape
    _, up_rows, hd = up.shape
    pairs = ((up_hbm, up), (down_hbm, down), (prompt_hbm.at[0], key_out), (prompt_hbm.at[1], value_out))
    loads = [pltpu.make_async_copy(a, b, sems.at[i]) for i, (a, b) in enumerate(pairs)]
    for c in loads:
        c.start()
    for c in loads:
        c.wait()
    for a in range(adapt_n):
        down_out[a] = adapter_scale * down[a * rank : (a + 1) * rank, :]
        for h in range(up_out.shape[2] // hd):
            for r in range(0, rank, min(rank, up_rows)):
                at = (h * adapt_n + a) * rank + r
                begin = at % up_rows
                size = min(rank, up_rows)
                up_out[a, r : r + size, h * hd : (h + 1) * hd] = (
                    adapter_scale * up[at // up_rows, begin : begin + size, :]
                )


def finish(up_w, down, up, prompt):
    adapt_n, rank, feature_n = up_w.shape
    f32 = jnp.float32
    spec = pl.BlockSpec(memory_space=VMEM)
    side = jax.ShapeDtypeStruct(prompt.shape[1:], f32)
    return pl.pallas_call(
        finish_kernel,
        out_shape=(
            jax.ShapeDtypeStruct((adapt_n, rank, down.shape[1]), f32),
            jax.ShapeDtypeStruct(up_w.shape, f32),
            side,
            side,
        ),
        in_specs=[pl.BlockSpec(memory_space=pl.ANY)] * 3,
        out_specs=(spec,) * 4,
        scratch_shapes=[VMEM(down.shape, f32), VMEM(up.shape, f32), pltpu.SemaphoreType.DMA((4,))],
        name="finish",
    )(down, up, prompt)


def local(
    hidden,
    response_base_queries,
    attention_output_gradient,
    keys,
    values,
    adapter_down_weight,
    adapter_up_weight,
    lengths,
    offsets,
):
    n = lax.axis_size("seq")
    nz = lax.axis_size("adapter")
    sums = gradients(
        n,
        nz,
        hidden,
        response_base_queries,
        attention_output_gradient,
        adapter_down_weight,
        adapter_up_weight,
        lengths,
        offsets,
        keys,
        values,
    )
    return finish(adapter_up_weight, *sums)


def solution(mesh):
    return jax.shard_map(
        local,
        mesh=mesh,
        in_specs=(
            P("adapter", "seq", None),
            P("adapter", "seq", None),
            P("adapter", "seq", None),
            P("seq", None),
            P("seq", None),
            P("adapter", None, None),
            P("adapter", None, None),
            P("adapter"),
            P("adapter", "seq"),
        ),
        out_specs=(
            P("adapter", None, "seq"),
            P("adapter", None, None),
            P(("seq", "adapter"), None),
            P(("seq", "adapter"), None),
        ),
        check_vma=False,
    )
```

profile of v0, /device:TPU:0, one launch (start us, length us, event | category | flops | bytes accessed | tf_op | source)
XLA Modules:
  0.0 62.1 jit_solution(2046601170386470521)
XLA Ops:
  0.6 59.6 %gradients.1 = (f32[32,1024]{1,0:T(8,128)}, f32[8,32,128]{2,1,0:T(8,128)}, f32[2,192,128]{2,1,0:T(8,128)}) custom-call(s32[2]{0:T(128)} %len_ref.1, bf16[2,128,8192]{2,1,0:T(8,128)(2,1)} %hidden_hbm.1, bf16[2,128,1024]{2,1,0:T(8,128)(2,1)} %base_hbm.1, bf16[2,128,1024]{2,1,0:T(8,128)(2,1)} %grad_hbm.1, bf16[2,16,8192]{2,1,0:T(8,128)(2,1)} %down_w.1, ...), custom_call_target="tpu_custom_call" | custom-call | tf_op jit(solution)/shard_map/gradients/pallas_call | solution.py:461
  60.2 1.9 %finish.1 = (f32[2,16,1024]{2,1,0:T(8,128)}, f32[2,16,1024]{2,1,0:T(8,128)}, f32[192,128]{1,0:T(8,128)}, f32[192,128]{1,0:T(8,128)}) custom-call(f32[32,1024]{1,0:T(8,128)} %get-tuple-element.7.down_hbm, f32[8,32,128]{2,1,0:T(8,128)} %get-tuple-element.8.up_hbm, f32[2,192,128]{2,1,0:T(8,128)} %get-tuple-element.9.prompt_hbm), custom_call_target="tpu_custom_call" | custom-call | tf_op jit(solution)/shard_map/finish/pallas_call | solution.py:534
where the time goes:
time: 63.2 us; the launch traced here: 62.1 us
  Pallas kernels  61.4 us (97%)
  between operations  0.64 us (1%)
    pallas_call x1, Pallas kernels, gradients(): pl.pallas_call(functools.partial(attend_kernel, n, nz, heads, chunk), out...  59.6 us
    pallas_call x1, Pallas kernels, finish(): pl.pallas_call(finish_kernel, out_shape=(jax.ShapeDtypeStruct((adapt_n, r...  1.87 us

commit v1 on v0

--- a/solution.py
+++ b/solution.py
@@ -35,8 +35,8 @@
     n, nz, heads, chunk,
     len_ref, hidden_hbm, base_hbm, grad_hbm, down_w, up_w, offset_ref, keys_ref, values_ref,
     down_out, up_out, prompt_out,
-    low_ref, dq_ref, part, hidden, base, grad, q_all, g_all, k_all, v_all, kt, s_ref, p_ref, peaks, place_ref,
-    key_acc, value_acc, prob_all, ds_all, load_sem, send_sem, recv_sem,
+    low_ref, dq_ref, part, hidden, base, grad, gq_all, k_all, v_all, kt, s_ref, dp_ref, peaks, totals, inners,
+    weight, delta, place_ref, acc, dq_acc, load_sem, send_sem, recv_sem,
     down, up, pair_a, pair_b, back_two, back_three, summed, total, z_in, down_in, up_in, up_mine,
     pair_send, pair_recv, back_send, back_recv, z_send, z_recv, d_send, d_recv, u_send, u_recv,
     ag_send, ag_recv,
@@ -46,7 +46,7 @@
     partner = s + 1 - 2 * core
     adapt_n, rows, _ = base.shape
     stretch, hd = keys_ref.shape
-    tiles, wide, _ = q_all.shape
+    tiles, wide, _ = gq_all.shape
     per = tiles // adapt_n
     factor = hd**-0.5
     pieces = stretch // chunk
@@ -122,8 +122,6 @@
             k_all[slot] = jnp.zeros(k_all.shape[1:], k_all.dtype)
             v_all[slot] = jnp.zeros(v_all.shape[1:], v_all.dtype)
 
-    key_acc[...] = jnp.zeros_like(key_acc)
-    value_acc[...] = jnp.zeros_like(value_acc)
     for c in loads:
         c.wait()
     for a in range(adapt_n):
@@ -138,8 +136,8 @@
         g = jnp.where(live, grad[a], jnp.zeros_like(grad[a]))
         for h in range(per * heads):
             t, at_row = a * per + h // heads, (h % heads) * rows
-            q_all[t, at_row : at_row + rows, :] = query[:, h * hd : (h + 1) * hd]
-            g_all[t, at_row : at_row + rows, :] = g[:, h * hd : (h + 1) * hd]
+            gq_all[t, at_row : at_row + rows, :hd] = g[:, h * hd : (h + 1) * hd]
+            gq_all[t, at_row : at_row + rows, hd:] = query[:, h * hd : (h + 1) * hd]
 
     def hand(i):
         @pl.when(s >= 2)
@@ -159,23 +157,57 @@
         pos = piece * chunk + lax.broadcasted_iota(jnp.int32, (chunk, wide), 0)
         return pos <= place
 
+    spots = {0: 0, 3: 1, 1: 2, 2: 3}
+
     def turned(d):
-        kt[:, d * stretch : (d + 1) * stretch] = k_all[d].T
-
-    peaks[...] = jnp.full(peaks.shape, masked_score, jnp.float32)
+        kt[:, spots[d] * stretch : (spots[d] + 1) * stretch] = k_all[d].T
+
+    def product(source, d, piece, other):
+        return dot(source[d, at(piece), :], other, ((1,), (1,)))
+
+    far_bias = jnp.where(s >= 3, 0.0, masked_score)
+
+    @pl.loop(0, tiles)
+    def _(t):
+        q = gq_all[t, :, hd:]
+        g = gq_all[t, :, :hd]
+        for piece in range(pieces):
+            s_ref[t, at(piece), :] = product(k_all, 0, piece, q) * factor
+            dp_ref[t, at(piece), :] = product(v_all, 0, piece, g)
 
     def scores_of(d):
-        bias = jnp.where(s >= d, 0.0, masked_score)
-
         @pl.loop(0, tiles)
         def _(t):
-            q = q_all[t]
-            peak = peaks[t]
+            q = gq_all[t, :, hd:]
+            peak = jnp.full((1, wide), masked_score, jnp.float32)
             for piece in range(pieces):
-                score = dot(k_all[d, at(piece), :], q, ((1,), (1,))) * factor + bias
+                score = product(k_all, d or 3, piece, q) * factor
+                if d == 0:
+                    near = before(piece, place_ref[t])
+                    score = jnp.where(near, s_ref[t, at(piece), :], score + far_bias)
                 s_ref[t, at(d * pieces + piece), :] = score
                 peak = jnp.maximum(peak, jnp.max(score, axis=0, keepdims=True))
-            peaks[t] = peak
+            peaks[d, t] = peak
+
+    def raise_of(d):
+        @pl.loop(0, tiles)
+        def _(t):
+            g = gq_all[t, :, :hd]
+            peak = peaks[d, t]
+            total = jnp.zeros((1, wide), jnp.float32)
+            inner = jnp.zeros((1, wide), jnp.float32)
+            for piece in range(pieces):
+                spot = at(d * pieces + piece)
+                e = jnp.exp(s_ref[t, spot, :] - peak)
+                dp = product(v_all, d or 3, piece, g)
+                if d == 0:
+                    dp = jnp.where(before(piece, place_ref[t]), dp_ref[t, spot, :], dp)
+                s_ref[t, spot, :] = e
+                dp_ref[t, spot, :] = dp
+                total = total + jnp.sum(e, axis=0, keepdims=True)
+                inner = inner + jnp.sum(e * dp, axis=0, keepdims=True)
+            totals[d, t] = total
+            inners[d, t] = inner
 
     arrived(2, 0)
     hand(0)
@@ -186,75 +218,70 @@
     scores_of(1)
     arrived(2, 1)
     hand(1)
+    raise_of(2)
+    arrived(1, 1)
+    raise_of(1)
     arrived(3, 0)
     turned(3)
     turned(0)
-    far = jnp.where(s >= 3, 1.0, 0.0)
-    far_bias = jnp.where(s >= 3, 0.0, masked_score)
+    scores_of(0)
+    arrived(3, 1)
+    raise_of(0)
 
     @pl.loop(0, tiles)
     def _(t):
-        q = q_all[t]
-        peak = peaks[t]
-        place = place_ref[t]
-        for piece in range(pieces):
-            near = dot(k_all[0, at(piece), :], q, ((1,), (1,))) * factor
-            other = dot(k_all[3, at(piece), :], q, ((1,), (1,))) * (factor * far) + far_bias
-            score = jnp.where(before(piece, place), near, other)
-            s_ref[t, at(piece), :] = score
-            peak = jnp.maximum(peak, jnp.max(score, axis=0, keepdims=True))
-        peaks[t] = peak
-
-    arrived(1, 1)
-    arrived(3, 1)
-    units = [(0, piece) for piece in range(pieces)]
-    units += [(d, piece) for d in (1, 2) for piece in range(pieces)]
-
-    @pl.loop(0, tiles)
-    def _(t):
-        q = q_all[t]
-        g = g_all[t]
-        peak = peaks[t]
-        place = place_ref[t]
+        tops = [peaks[0, t]] + [jnp.where(s >= d, peaks[d, t], masked_score) for d in (1, 2)]
+        peak = jnp.maximum(jnp.maximum(tops[0], tops[1]), tops[2])
+        shares = [jnp.exp(top - peak) for top in tops]
         total = jnp.zeros((1, wide), jnp.float32)
         inner = jnp.zeros((1, wide), jnp.float32)
-        for u, (d, piece) in enumerate(units):
-            e = jnp.exp(s_ref[t, at(u), :] - peak)
-            dp = dot(v_all[d, at(piece), :], g, ((1,), (1,)))
-            if d == 0:
-                other = dot(v_all[3, at(piece), :], g, ((1,), (1,)))
-                dp = jnp.where(before(piece, place), dp, other)
-            s_ref[t, at(u), :] = e
-            p_ref[at(u), :] = dp
-            total = total + jnp.sum(e, axis=0, keepdims=True)
-            inner = inner + jnp.sum(e * dp, axis=0, keepdims=True)
+        for d, share in enumerate(shares):
+            total = total + totals[d, t] * share
+            inner = inner + inners[d, t] * share
         inverse = 1.0 / total
-        delta = inner * inverse
-        dq = jnp.zeros((hd, wide), jnp.float32)
-        for u, (d, piece) in enumerate(units):
-            prob = s_ref[t, at(u), :] * inverse
-            ds = prob * (p_ref[at(u), :] - delta)
-            if d == 0:
-                near = before(piece, place)
-                cases = [
-                    (0, jnp.where(near, prob, 0.0), jnp.where(near, ds, 0.0)),
-                    (3, jnp.where(near, 0.0, prob), jnp.where(near, 0.0, ds)),
-                ]
-            else:
-                cases = [(d, prob, ds)]
-            for block, prob_part, ds_part in cases:
-                prob_low = prob_part.astype(jnp.bfloat16)
-                ds_low = ds_part.astype(jnp.bfloat16)
+        for d, share in enumerate(shares):
+            weight[d, t] = share * inverse
+        delta[t] = inner * inverse
+
+    def split(piece, t, d, value):
+        if d:
+            return [value.astype(jnp.bfloat16)]
+        near = before(piece, place_ref[t])
+        return [
+            jnp.where(near, value, 0.0).astype(jnp.bfloat16),
+            jnp.where(near, 0.0, value).astype(jnp.bfloat16),
+        ]
+
+    def gather_up(d, i):
+        acc[...] = jnp.zeros_like(acc)
+        blocks = (d,) if d else (0, 3)
+
+        @pl.loop(0, tiles)
+        def _(t):
+            other = gq_all[t]
+            share = weight[d, t]
+            lows = [[] for _ in blocks]
+            for piece in range(pieces):
+                spot = at(d * pieces + piece)
+                value = s_ref[t, spot, :] * share
+                if i == 0:
+                    value = value * (dp_ref[t, spot, :] - delta[t])
+                for j, low in enumerate(split(piece, t, d, value)):
+                    both = dot(low, other, ((1,), (0,)))
+                    acc[j, at(piece), :] += both[:, :hd] if i else both[:, hd:]
+                    lows[j].append(low)
+            if i == 0:
+                begin = spots[d] * stretch
+                ds = jnp.concatenate(sum(lows, []), axis=0)
+                dq = dot(kt[:, begin : begin + len(blocks) * stretch], ds, ((1,), (0,)))
                 if d == 0:
-                    value_acc[block // 3, at(piece), :] += dot(prob_low, g, ((1,), (0,)))
-                    key_acc[block // 3, at(piece), :] += dot(ds_low, q, ((1,), (0,)))
+                    dq_acc[t] = dq
                 else:
-                    columns = pl.ds(pl.multiple_of(t * wide, 128), wide)
-                    prob_all[at(u - pieces), columns] = prob_low
-                    ds_all[at(u - pieces), columns] = ds_low
-                begin = block * stretch + piece * chunk
-                dq = dq + dot(kt[:, begin : begin + chunk], ds_low, ((1,), (0,)))
-        dq_ref[t] = (dq * factor).T.astype(jnp.bfloat16)
+                    dq_acc[t] += dq
+
+        for j, block in enumerate(blocks):
+            out = acc[j]
+            part[block, i] = (out if i else out * factor).astype(jnp.bfloat16)
 
     width = down_out.shape[1]
     quarter = prompt_out.shape[1]
@@ -274,19 +301,6 @@
         remote(summed.at[i], back_two.at[i], back_send.at[0, i], back_recv.at[0, i], to_seq(s - 2))
         for i in range(2)
     ]
-    def summed_up(d, i):
-        for piece in range(pieces):
-            if d in (0, 3):
-                if i == 0:
-                    part[d, 0, at(piece), :] = (key_acc[d // 3, at(piece), :] * factor).astype(jnp.bfloat16)
-                else:
-                    part[d, 1, at(piece), :] = value_acc[d // 3, at(piece), :].astype(jnp.bfloat16)
-                continue
-            weights = (ds_all, prob_all)[i][at((d - 1) * pieces + piece), :]
-            other = (q_all, g_all)[i][...].reshape(tiles * wide, hd)
-            out = dot(weights, other, ((1,), (0,)))
-            part[d, i, at(piece), :] = (out if i else out * factor).astype(jnp.bfloat16)
-
     downs, ups, gathers = [], [], []
     for i in range(1, n):
         peer = (s + i) % n
@@ -305,9 +319,44 @@
         def _():
             two_back[i].start()
 
-    for i in (1, 0):
-        summed_up(3, i)
-
+    spread = [[], []]
+
+    def owner(i):
+        @pl.when(core == 0)
+        def _():
+            near_back[i].wait_recv()
+
+        @pl.when(s + 2 < n)
+        def _():
+            two_back[i].wait_recv()
+
+        @pl.when(has_three_in)
+        def _():
+            far_back[i].wait_recv()
+
+        total[i] = (
+            part[0, i].astype(jnp.float32)
+            + pair_b[i].astype(jnp.float32)
+            + back_two[i].astype(jnp.float32)
+            + back_three[i].astype(jnp.float32)
+        ).astype(jnp.bfloat16)
+        for j in range(1, nz):
+            peer = (z + j) % nz
+            c = remote(
+                total.at[i, pl.ds(pl.multiple_of(peer * quarter, 16), quarter), :],
+                z_in.at[j - 1, i], z_send.at[j - 1, i], z_recv.at[j - 1, i], to_adapter(peer),
+            )
+            c.start()
+            spread[i].append(c)
+
+    def prompt_sum(i):
+        mine = total[i, pl.ds(pl.multiple_of(z * quarter, 16), quarter), :].astype(jnp.float32)
+        for j, c in enumerate(spread[i]):
+            c.wait_recv()
+            mine = mine + z_in[j, i].astype(jnp.float32)
+        prompt_out[i] = mine
+
+    def far_out(i):
         @pl.when(core == 1)
         def _():
             one_to_zero[i].start()
@@ -316,9 +365,7 @@
         def _():
             far_back[i].start()
 
-    for i in (1, 0):
-        summed_up(1, i)
-
+    def near_out(i):
         @pl.when(core == 0)
         def _():
             zero_to_one[i].start()
@@ -327,8 +374,30 @@
         def _():
             near_back[i].start()
 
-        summed_up(2, i)
-        sum_pair(i)
+    def sum_on(which, i):
+        @pl.when(core == which)
+        def _():
+            sum_pair(i)
+
+    gather_up(0, 1)
+    far_out(1)
+    gather_up(2, 1)
+    sum_on(0, 1)
+    gather_up(1, 1)
+    near_out(1)
+    gather_up(0, 0)
+    far_out(0)
+    sum_on(1, 1)
+    gather_up(2, 0)
+    sum_on(0, 0)
+    owner(1)
+    gather_up(1, 0)
+    near_out(0)
+
+    @pl.loop(0, tiles)
+    def _(t):
+        dq_ref[t] = (dq_acc[t] * factor).T.astype(jnp.bfloat16)
+
     _, rank, feature_n = up_w.shape
     group = feature_n // hd
     shards, up_rows, _ = up.shape
@@ -346,48 +415,11 @@
         down[a * rank : (a + 1) * rank, :] = dot(
             small.astype(jnp.bfloat16), hidden[a], ((0,), (0,))
         ).astype(jnp.bfloat16)
+        if a == 0:
+            sum_on(1, 0)
     for c in ups + downs:
         c.start()
-    spread = [[], []]
-    summed_up(0, 1)
-    summed_up(0, 0)
-
-    def owner(i):
-        @pl.when(core == 0)
-        def _():
-            near_back[i].wait_recv()
-
-        @pl.when(s + 2 < n)
-        def _():
-            two_back[i].wait_recv()
-
-        @pl.when(has_three_in)
-        def _():
-            far_back[i].wait_recv()
-
-        total[i] = (
-            part[0, i].astype(jnp.float32)
-            + pair_b[i].astype(jnp.float32)
-            + back_two[i].astype(jnp.float32)
-            + back_three[i].astype(jnp.float32)
-        ).astype(jnp.bfloat16)
-        for j in range(1, nz):
-            peer = (z + j) % nz
-            c = remote(
-                total.at[i, pl.ds(pl.multiple_of(peer * quarter, 16), quarter), :],
-                z_in.at[j - 1, i], z_send.at[j - 1, i], z_recv.at[j - 1, i], to_adapter(peer),
-            )
-            c.start()
-            spread[i].append(c)
-
-    def prompt_sum(i):
-        mine = total[i, pl.ds(pl.multiple_of(z * quarter, 16), quarter), :].astype(jnp.float32)
-        for j, c in enumerate(spread[i]):
-            c.wait_recv()
-            mine = mine + z_in[j, i].astype(jnp.float32)
-        prompt_out[i] = mine
-
-    owner(1)
+    owner(0)
     mine = up[s]
     for i, c in enumerate(ups):
         c.wait_recv()
@@ -396,7 +428,6 @@
     for c in gathers:
         c.start()
     up_out[s] = mine
-    owner(0)
     mine = down[:, pl.ds(pl.multiple_of(s * width, 128), width)].astype(jnp.float32)
     for i, c in enumerate(downs):
         c.wait_recv()
@@ -458,6 +489,7 @@
     bf16 = jnp.bfloat16
     f32 = jnp.float32
     block = VMEM((2, stretch, hd), bf16)
+    stat = VMEM((3, tiles, 1, wide), f32)
     return pl.pallas_call(
         functools.partial(attend_kernel, n, nz, heads, chunk),
         out_shape=(
@@ -474,19 +506,17 @@
             VMEM(hidden.shape, bf16),
             VMEM(base.shape, bf16),
             VMEM(grad.shape, bf16),
-            VMEM((tiles, wide, hd), bf16),
-            VMEM((tiles, wide, hd), bf16),
+            VMEM((tiles, wide, 2 * hd), bf16),
             VMEM((4, stretch, hd), bf16),
             VMEM((4, stretch, hd), bf16),
             VMEM((hd, 4 * stretch), bf16),
             VMEM((tiles, 3 * stretch, wide), f32),
-            VMEM((3 * stretch, wide), f32),
+            VMEM((tiles, 3 * stretch, wide), f32),
+            stat, stat, stat, stat,
             VMEM((tiles, 1, wide), f32),
             VMEM((tiles, 1, wide), jnp.int32),
             VMEM((2, stretch, hd), f32),
-            VMEM((2, stretch, hd), f32),
-            VMEM((2 * stretch, tiles * wide), bf16),
-            VMEM((2 * stretch, tiles * wide), bf16),
+            VMEM((tiles, hd, wide), f32),
             dma((3,)), dma((3, 2)), dma((4, 2)),
             VMEM((ranks, model), bf16),
             VMEM(up_shape, f32),

time: 63.2 us -> 58.1 us (0.919); the launches traced: 62.1 us -> 58 us
  Pallas kernels: 61.4 us -> 57.3 us
    pallas_call x1, Pallas kernels: 59.6 us -> 55.5 us  [gradients(): pl.pallas_call(functools.partial(attend_kernel, n, nz, heads, chunk), out...]
where the time goes in v1:
time: 58.1 us; the launch traced here: 58 us
  Pallas kernels  57.3 us (99%)
  between operations  0.64 us (1%)
    pallas_call x1, Pallas kernels, gradients(): pl.pallas_call(functools.partial(attend_kernel, n, nz, heads, chunk), out...  55.5 us
    pallas_call x1, Pallas kernels, finish(): pl.pallas_call(finish_kernel, out_shape=(jax.ShapeDtypeStruct((adapt_n, r...  1.87 us

profile of v1, /device:TPU:0, one launch (start us, length us, event | category | flops | bytes accessed | tf_op | source)
XLA Modules:
  0.0 58.0 jit_solution(17415671227919159521)
XLA Ops:
  0.6 55.5 %gradients.1 = (f32[32,1024]{1,0:T(8,128)}, f32[8,32,128]{2,1,0:T(8,128)}, f32[2,192,128]{2,1,0:T(8,128)}) custom-call(s32[2]{0:T(128)} %len_ref.1, bf16[2,128,8192]{2,1,0:T(8,128)(2,1)} %hidden_hbm.1, bf16[2,128,1024]{2,1,0:T(8,128)(2,1)} %base_hbm.1, bf16[2,128,1024]{2,1,0:T(8,128)(2,1)} %grad_hbm.1, bf16[2,16,8192]{2,1,0:T(8,128)(2,1)} %down_w.1, ...), custom_call_target="tpu_custom_call" | custom-call | tf_op jit(solution)/shard_map/gradients/pallas_call | solution.py:493
  56.1 1.9 %finish.1 = (f32[2,16,1024]{2,1,0:T(8,128)}, f32[2,16,1024]{2,1,0:T(8,128)}, f32[192,128]{1,0:T(8,128)}, f32[192,128]{1,0:T(8,128)}) custom-call(f32[32,1024]{1,0:T(8,128)} %get-tuple-element.7.down_hbm, f32[8,32,128]{2,1,0:T(8,128)} %get-tuple-element.8.up_hbm, f32[2,192,128]{2,1,0:T(8,128)} %get-tuple-element.9.prompt_hbm), custom_call_target="tpu_custom_call" | custom-call | tf_op jit(solution)/shard_map/finish/pallas_call | solution.py:564

commit v2 on v1

--- a/solution.py
+++ b/solution.py
@@ -243,44 +243,47 @@
             weight[d, t] = share * inverse
         delta[t] = inner * inverse
 
-    def split(piece, t, d, value):
-        if d:
-            return [value.astype(jnp.bfloat16)]
-        near = before(piece, place_ref[t])
-        return [
-            jnp.where(near, value, 0.0).astype(jnp.bfloat16),
-            jnp.where(near, 0.0, value).astype(jnp.bfloat16),
-        ]
-
-    def gather_up(d, i):
-        acc[...] = jnp.zeros_like(acc)
-        blocks = (d,) if d else (0, 3)
-
-        @pl.loop(0, tiles)
+    def rows_of(unit, piece):
+        if isinstance(unit, int):
+            return at(unit * pieces + piece)
+        return pl.ds(pl.multiple_of(unit * stretch + piece * chunk, chunk), chunk)
+
+    def gather_up(block, i, first=0, last=tiles):
+        static = isinstance(block, int)
+        unit = 0 if static else block
+        if first == 0:
+            acc[...] = jnp.zeros_like(acc)
+
+        @pl.loop(first, last)
         def _(t):
             other = gq_all[t]
-            share = weight[d, t]
-            lows = [[] for _ in blocks]
+            share = weight[unit, t]
+            lows = []
             for piece in range(pieces):
-                spot = at(d * pieces + piece)
+                spot = rows_of(unit, piece)
                 value = s_ref[t, spot, :] * share
                 if i == 0:
                     value = value * (dp_ref[t, spot, :] - delta[t])
-                for j, low in enumerate(split(piece, t, d, value)):
-                    both = dot(low, other, ((1,), (0,)))
-                    acc[j, at(piece), :] += both[:, :hd] if i else both[:, hd:]
-                    lows[j].append(low)
+                if static:
+                    near = before(piece, place_ref[t])
+                    value = jnp.where(near, 0.0, value) if block else jnp.where(near, value, 0.0)
+                low = value.astype(jnp.bfloat16)
+                both = dot(low, other, ((1,), (0,)))
+                acc[at(piece), :] += both[:, :hd] if i else both[:, hd:]
+                lows.append(low)
             if i == 0:
-                begin = spots[d] * stretch
-                ds = jnp.concatenate(sum(lows, []), axis=0)
-                dq = dot(kt[:, begin : begin + len(blocks) * stretch], ds, ((1,), (0,)))
-                if d == 0:
+                if static:
+                    turned_block = kt[:, spots[block] * stretch : (spots[block] + 1) * stretch]
+                else:
+                    turned_block = kt[:, pl.ds(pl.multiple_of((block + 1) * stretch, stretch), stretch)]
+                dq = dot(turned_block, jnp.concatenate(lows, axis=0), ((1,), (0,)))
+                if static and block == 3:
                     dq_acc[t] = dq
                 else:
                     dq_acc[t] += dq
 
-        for j, block in enumerate(blocks):
-            out = acc[j]
+        if last == tiles:
+            out = acc[...]
             part[block, i] = (out if i else out * factor).astype(jnp.bfloat16)
 
     width = down_out.shape[1]
@@ -365,34 +368,43 @@
         def _():
             far_back[i].start()
 
-    def near_out(i):
-        @pl.when(core == 0)
-        def _():
-            zero_to_one[i].start()
-
-        @pl.when(core == 1)
-        def _():
-            near_back[i].start()
-
     def sum_on(which, i):
         @pl.when(core == which)
         def _():
             sum_pair(i)
 
+    second = 1 + core
+    third = 2 - core
+    middle = tiles // 2
+
+    def second_out(i):
+        gather_up(second, i)
+
+        @pl.when(core == 0)
+        def _():
+            zero_to_one[i].start()
+
+    def third_out(i):
+        gather_up(third, i, 0, middle)
+        sum_on(1, i)
+        gather_up(third, i, middle, tiles)
+        sum_on(0, i)
+
+        @pl.when(core == 1)
+        def _():
+            near_back[i].start()
+
+    gather_up(3, 1)
+    far_out(1)
+    second_out(1)
+    third_out(1)
+    gather_up(3, 0)
+    far_out(0)
     gather_up(0, 1)
-    far_out(1)
-    gather_up(2, 1)
-    sum_on(0, 1)
-    gather_up(1, 1)
-    near_out(1)
+    second_out(0)
+    owner(1)
+    third_out(0)
     gather_up(0, 0)
-    far_out(0)
-    sum_on(1, 1)
-    gather_up(2, 0)
-    sum_on(0, 0)
-    owner(1)
-    gather_up(1, 0)
-    near_out(0)
 
     @pl.loop(0, tiles)
     def _(t):
@@ -401,6 +413,7 @@
     _, rank, feature_n = up_w.shape
     group = feature_n // hd
     shards, up_rows, _ = up.shape
+    smalls = []
     for a in range(adapt_n):
         small = jnp.zeros((rows, rank), jnp.float32)
         for h in range(group):
@@ -412,22 +425,20 @@
                 begin = spot % up_rows
                 up[spot // up_rows, begin : begin + min(rank, up_rows), :] = up_h[r : r + min(rank, up_rows)]
             small = small + dot(dq_h, up_w[a, :, h * hd : (h + 1) * hd], ((1,), (1,)))
-        down[a * rank : (a + 1) * rank, :] = dot(
-            small.astype(jnp.bfloat16), hidden[a], ((0,), (0,))
-        ).astype(jnp.bfloat16)
-        if a == 0:
-            sum_on(1, 0)
-    for c in ups + downs:
+        smalls.append(small.astype(jnp.bfloat16))
+    for c in ups:
         c.start()
-    owner(0)
+    for a in range(adapt_n):
+        down[a * rank : (a + 1) * rank, :] = dot(smalls[a], hidden[a], ((0,), (0,))).astype(jnp.bfloat16)
     mine = up[s]
     for i, c in enumerate(ups):
         c.wait_recv()
         mine = mine + up_in[i]
     up_mine[...] = mine
-    for c in gathers:
+    for c in gathers + downs:
         c.start()
     up_out[s] = mine
+    owner(0)
     mine = down[:, pl.ds(pl.multiple_of(s * width, 128), width)].astype(jnp.float32)
     for i, c in enumerate(downs):
         c.wait_recv()
@@ -515,7 +526,7 @@
             stat, stat, stat, stat,
             VMEM((tiles, 1, wide), f32),
             VMEM((tiles, 1, wide), jnp.int32),
-            VMEM((2, stretch, hd), f32),
+            VMEM((stretch, hd), f32),
             VMEM((tiles, hd, wide), f32),
             dma((3,)), dma((3, 2)), dma((4, 2)),
             VMEM((ranks, model), bf16),

time: 58.1 us -> 58.7 us (1.010)
  no operation moved by 1% of the time
where the time goes in v2:
time: 58.7 us; the launch traced here: 58.3 us
  Pallas kernels  57.7 us (98%)
  between operations  0.64 us (1%)
    pallas_call x1, Pallas kernels, gradients(): pl.pallas_call(functools.partial(attend_kernel, n, nz, heads, chunk), out...  55.8 us
    pallas_call x1, Pallas kernels, finish(): pl.pallas_call(finish_kernel, out_shape=(jax.ShapeDtypeStruct((adapt_n, r...  1.87 us

profile of v2, /device:TPU:0, one launch (start us, length us, event | category | flops | bytes accessed | tf_op | source)
XLA Modules:
  0.0 58.3 jit_solution(16531952365194925893)
XLA Ops:
  0.6 55.8 %gradients.1 = (f32[32,1024]{1,0:T(8,128)}, f32[8,32,128]{2,1,0:T(8,128)}, f32[2,192,128]{2,1,0:T(8,128)}) custom-call(s32[2]{0:T(128)} %len_ref.1, bf16[2,128,8192]{2,1,0:T(8,128)(2,1)} %hidden_hbm.1, bf16[2,128,1024]{2,1,0:T(8,128)(2,1)} %base_hbm.1, bf16[2,128,1024]{2,1,0:T(8,128)(2,1)} %grad_hbm.1, bf16[2,16,8192]{2,1,0:T(8,128)(2,1)} %down_w.1, ...), custom_call_target="tpu_custom_call" | custom-call | tf_op jit(solution)/shard_map/gradients/pallas_call | solution.py:504
  56.5 1.9 %finish.1 = (f32[2,16,1024]{2,1,0:T(8,128)}, f32[2,16,1024]{2,1,0:T(8,128)}, f32[192,128]{1,0:T(8,128)}, f32[192,128]{1,0:T(8,128)}) custom-call(f32[32,1024]{1,0:T(8,128)} %get-tuple-element.7.down_hbm, f32[8,32,128]{2,1,0:T(8,128)} %get-tuple-element.8.up_hbm, f32[2,192,128]{2,1,0:T(8,128)} %get-tuple-element.9.prompt_hbm), custom_call_target="tpu_custom_call" | custom-call | tf_op jit(solution)/shard_map/finish/pallas_call | solution.py:575

commit v3 on v2

--- a/solution.py
+++ b/solution.py
@@ -37,9 +37,9 @@
     down_out, up_out, prompt_out,
     low_ref, dq_ref, part, hidden, base, grad, gq_all, k_all, v_all, kt, s_ref, dp_ref, peaks, totals, inners,
     weight, delta, place_ref, acc, dq_acc, load_sem, send_sem, recv_sem,
-    down, up, pair_a, pair_b, back_two, back_three, summed, total, z_in, down_in, up_in, up_mine,
-    pair_send, pair_recv, back_send, back_recv, z_send, z_recv, d_send, d_recv, u_send, u_recv,
-    ag_send, ag_recv,
+    down, up, pair_a, pair_b, back_two, back_three, summed, total, z_in, down_pair, down_chip, down_in,
+    up_pair, up_all, pair_send, pair_recv, back_send, back_recv, z_send, z_recv, d_send, d_recv, u_send, u_recv,
+    swap_send, swap_recv,
 ):
     s = lax.axis_index("seq")
     core = s % 2
@@ -286,7 +286,6 @@
             out = acc[...]
             part[block, i] = (out if i else out * factor).astype(jnp.bfloat16)
 
-    width = down_out.shape[1]
     quarter = prompt_out.shape[1]
     has_far = (core == 0) & (s >= 3)
 
@@ -304,15 +303,17 @@
         remote(summed.at[i], back_two.at[i], back_send.at[0, i], back_recv.at[0, i], to_seq(s - 2))
         for i in range(2)
     ]
-    downs, ups, gathers = [], [], []
-    for i in range(1, n):
-        peer = (s + i) % n
-        columns = pl.ds(pl.multiple_of(peer * width, 128), width)
-        downs.append(
-            remote(down.at[:, columns], down_in.at[i - 1], d_send.at[i - 1], d_recv.at[i - 1], to_seq(peer))
-        )
-        ups.append(remote(up.at[peer], up_in.at[i - 1], u_send.at[i - 1], u_recv.at[i - 1], to_seq(peer)))
-        gathers.append(remote(up_mine, up_out.at[s], ag_send.at[i - 1], ag_recv.at[i - 1], to_seq(peer)))
+    chips = n // 2
+    chip = s // 2
+    down_swap = remote(down.at[1 - core], down_pair, swap_send.at[0], swap_recv.at[0], to_seq(partner))
+    up_swap = remote(up.at[1 - core], up_pair, swap_send.at[1], swap_recv.at[1], to_seq(partner))
+    up_back = remote(up_out.at[core], up_out.at[core], swap_send.at[2], swap_recv.at[2], to_seq(partner))
+    downs, ups = [], []
+    for i in range(1, chips):
+        peer = (chip + i) % chips
+        target = to_seq(2 * peer + core)
+        downs.append(remote(down_chip.at[peer], down_in.at[i - 1], d_send.at[i - 1], d_recv.at[i - 1], target))
+        ups.append(remote(up_all.at[chip], up_all.at[chip], u_send.at[i - 1], u_recv.at[i - 1], target))
 
     def sum_pair(i):
         zero_to_one[i].wait_recv()
@@ -412,7 +413,8 @@
 
     _, rank, feature_n = up_w.shape
     group = feature_n // hd
-    shards, up_rows, _ = up.shape
+    half = feature_n // 2
+    width = down_out.shape[1]
     smalls = []
     for a in range(adapt_n):
         small = jnp.zeros((rows, rank), jnp.float32)
@@ -420,35 +422,43 @@
             place = a * group + h
             dq_h = dq_ref[place // heads, (place % heads) * rows : (place % heads + 1) * rows, :]
             up_h = dot(low_ref[a], dq_h, ((0,), (0,)))
-            for r in range(0, rank, min(rank, up_rows)):
-                spot = (h * adapt_n + a) * rank + r
-                begin = spot % up_rows
-                up[spot // up_rows, begin : begin + min(rank, up_rows), :] = up_h[r : r + min(rank, up_rows)]
+            begin = h * hd % half
+            up[h * hd // half, a * rank : (a + 1) * rank, begin : begin + hd] = up_h.astype(jnp.bfloat16)
             small = small + dot(dq_h, up_w[a, :, h * hd : (h + 1) * hd], ((1,), (1,)))
         smalls.append(small.astype(jnp.bfloat16))
+    up_swap.start()
+    for a in range(adapt_n):
+        out = dot(smalls[a], hidden[a], ((0,), (0,))).astype(jnp.bfloat16)
+        for j in range(n):
+            down[j % 2, j // 2, a * rank : (a + 1) * rank, :] = out[:, j * width : (j + 1) * width]
+    down_swap.start()
+    up_swap.wait_recv()
+    up_all[chip] = (up[core].astype(jnp.float32) + up_pair[...].astype(jnp.float32)).astype(jnp.bfloat16)
     for c in ups:
         c.start()
-    for a in range(adapt_n):
-        down[a * rank : (a + 1) * rank, :] = dot(smalls[a], hidden[a], ((0,), (0,))).astype(jnp.bfloat16)
-    mine = up[s]
-    for i, c in enumerate(ups):
+    down_swap.wait_recv()
+    for j in range(chips):
+        both = down[core, j].astype(jnp.float32) + down_pair[j].astype(jnp.float32)
+        down_chip[j] = both.astype(jnp.bfloat16)
+    for c in downs:
+        c.start()
+    owner(0)
+    for c in ups:
         c.wait_recv()
-        mine = mine + up_in[i]
-    up_mine[...] = mine
-    for c in gathers + downs:
-        c.start()
-    up_out[s] = mine
-    owner(0)
-    mine = down[:, pl.ds(pl.multiple_of(s * width, 128), width)].astype(jnp.float32)
+    mine = up_all[0].astype(jnp.float32)
+    for j in range(1, chips):
+        mine = mine + up_all[j].astype(jnp.float32)
+    up_out[core] = mine
+    up_back.start()
+    mine = down[core, chip].astype(jnp.float32) + down_pair[chip].astype(jnp.float32)
     for i, c in enumerate(downs):
         c.wait_recv()
         mine = mine + down_in[i].astype(jnp.float32)
     down_out[...] = mine
     prompt_sum(1)
     prompt_sum(0)
-    for c in gathers:
-        c.wait_recv()
-    for c in downs + ups + gathers + spread[0] + spread[1] + zero_to_one:
+    up_back.wait_recv()
+    for c in downs + ups + spread[0] + spread[1] + zero_to_one + [up_swap, down_swap, up_back]:
         c.wait_send()
     for i in range(2):
 
@@ -493,7 +503,8 @@
     tiles = adapt_n * feature_n // (hd * heads)
     chunk = 256 if stretch % 256 == 0 else stretch
     quarter = stretch // nz
-    up_shape = (n, ranks * feature_n // (n * hd), hd)
+    up_shape = (2, ranks, feature_n // 2)
+    down_shape = (n // 2, ranks, model // n)
     spec = pl.BlockSpec(memory_space=VMEM)
     anywhere = pl.BlockSpec(memory_space=pl.ANY)
     dma = pltpu.SemaphoreType.DMA
@@ -529,15 +540,17 @@
             VMEM((stretch, hd), f32),
             VMEM((tiles, hd, wide), f32),
             dma((3,)), dma((3, 2)), dma((4, 2)),
-            VMEM((ranks, model), bf16),
-            VMEM(up_shape, f32),
+            VMEM((2,) + down_shape, bf16),
+            VMEM(up_shape, bf16),
             block, block, block, block, block, block,
             VMEM((nz - 1, 2, quarter, hd), bf16),
-            VMEM((n - 1, ranks, model // n), bf16),
-            VMEM((n - 1,) + up_shape[1:], f32),
-            VMEM(up_shape[1:], f32),
+            VMEM(down_shape, bf16),
+            VMEM(down_shape, bf16),
+            VMEM((n // 2 - 1,) + down_shape[1:], bf16),
+            VMEM(up_shape[1:], bf16),
+            VMEM((n // 2,) + up_shape[1:], bf16),
             dma((2, 2)), dma((2, 2)), dma((2, 2)), dma((2, 2)), dma((nz - 1, 2)), dma((nz - 1, 2)),
-            dma((n - 1,)), dma((n - 1,)), dma((n - 1,)), dma((n - 1,)), dma((n - 1,)), dma((n - 1,)),
+            dma((n // 2 - 1,)), dma((n // 2 - 1,)), dma((n // 2 - 1,)), dma((n // 2 - 1,)), dma((3,)), dma((3,)),
         ],
         compiler_params=pltpu.CompilerParams(
             collective_id=0, has_side_effects=True, vmem_limit_bytes=60 * 1024 * 1024
@@ -548,7 +561,7 @@
 
 def finish_kernel(down_hbm, up_hbm, prompt_hbm, down_out, up_out, key_out, value_out, down, up, sems):
     adapt_n, rank, _ = down_out.shape
-    _, up_rows, hd = up.shape
+    half = up.shape[2]
     pairs = ((up_hbm, up), (down_hbm, down), (prompt_hbm.at[0], key_out), (prompt_hbm.at[1], value_out))
     loads = [pltpu.make_async_copy(a, b, sems.at[i]) for i, (a, b) in enumerate(pairs)]
     for c in loads:
@@ -557,14 +570,8 @@
         c.wait()
     for a in range(adapt_n):
         down_out[a] = adapter_scale * down[a * rank : (a + 1) * rank, :]
-        for h in range(up_out.shape[2] // hd):
-            for r in range(0, rank, min(rank, up_rows)):
-                at = (h * adapt_n + a) * rank + r
-                begin = at % up_rows
-                size = min(rank, up_rows)
-                up_out[a, r : r + size, h * hd : (h + 1) * hd] = (
-                    adapter_scale * up[at // up_rows, begin : begin + size, :]
-                )
+        for j in range(2):
+            up_out[a, :, j * half : (j + 1) * half] = adapter_scale * up[j, a * rank : (a + 1) * rank, :]
 
 
 def finish(up_w, down, up, prompt):

time: 58.7 us -> 53.7 us (0.915)
  Pallas kernels: 57.7 us -> 52.9 us
    pallas_call x1, Pallas kernels: 55.8 us -> 51 us  [gradients(): pl.pallas_call(functools.partial(attend_kernel, n, nz, heads, chunk), out...]
where the time goes in v3:
time: 53.7 us; the launch traced here: 53.5 us
  Pallas kernels  52.9 us (99%)
  between operations  0.64 us (1%)
    pallas_call x1, Pallas kernels, gradients(): pl.pallas_call(functools.partial(attend_kernel, n, nz, heads, chunk), out...  51 us
    pallas_call x1, Pallas kernels, finish(): pl.pallas_call(finish_kernel, out_shape=(jax.ShapeDtypeStruct((adapt_n, r...  1.87 us

profile of v3, /device:TPU:0, one launch (start us, length us, event | category | flops | bytes accessed | tf_op | source)
XLA Modules:
  0.0 53.5 jit_solution(13612306687343298398)
XLA Ops:
  0.6 51.0 %gradients.1 = (f32[32,1024]{1,0:T(8,128)}, f32[2,32,512]{2,1,0:T(8,128)}, f32[2,192,128]{2,1,0:T(8,128)}) custom-call(s32[2]{0:T(128)} %len_ref.1, bf16[2,128,8192]{2,1,0:T(8,128)(2,1)} %hidden_hbm.1, bf16[2,128,1024]{2,1,0:T(8,128)(2,1)} %base_hbm.1, bf16[2,128,1024]{2,1,0:T(8,128)(2,1)} %grad_hbm.1, bf16[2,16,8192]{2,1,0:T(8,128)(2,1)} %down_w.1, ...), custom_call_target="tpu_custom_call" | custom-call | tf_op jit(solution)/shard_map/gradients/pallas_call | solution.py:515
  51.6 1.9 %finish.1 = (f32[2,16,1024]{2,1,0:T(8,128)}, f32[2,16,1024]{2,1,0:T(8,128)}, f32[192,128]{1,0:T(8,128)}, f32[192,128]{1,0:T(8,128)}) custom-call(f32[32,1024]{1,0:T(8,128)} %get-tuple-element.7.down_hbm, f32[2,32,512]{2,1,0:T(8,128)} %get-tuple-element.8.up_hbm, f32[2,192,128]{2,1,0:T(8,128)} %get-tuple-element.9.prompt_hbm), custom_call_target="tpu_custom_call" | custom-call | tf_op jit(solution)/shard_map/finish/pallas_call | solution.py:582

commit v4 on v3

--- a/solution.py
+++ b/solution.py
@@ -33,31 +33,38 @@
 
 def attend_kernel(
     n, nz, heads, chunk,
-    len_ref, hidden_hbm, base_hbm, grad_hbm, down_w, up_w, offset_ref, keys_ref, values_ref,
-    down_out, up_out, prompt_out,
-    low_ref, dq_ref, part, hidden, base, grad, gq_all, k_all, v_all, kt, s_ref, dp_ref, peaks, totals, inners,
-    weight, delta, place_ref, acc, dq_acc, load_sem, send_sem, recv_sem,
+    len_hbm, hidden_hbm, base_hbm, grad_hbm, down_hbm, up_hbm, offset_hbm, keys_hbm, values_hbm,
+    down_result, up_result, prompt_result,
+    len_ref, down_w, up_w, offset_ref, down_out, up_out, prompt_out, low_ref, dq_ref, part, hidden, base, grad, gq_all, g_turned, q_turned, k_all, v_all, kt, s_ref, dp_ref, peaks, totals, inners,
+    weight, delta, place_ref, acc, dq_acc, load_sem, out_sem, send_sem, recv_sem,
     down, up, pair_a, pair_b, back_two, back_three, summed, total, z_in, down_pair, down_chip, down_in,
     up_pair, up_all, pair_send, pair_recv, back_send, back_recv, z_send, z_recv, d_send, d_recv, u_send, u_recv,
     swap_send, swap_recv,
 ):
     s = lax.axis_index("seq")
+    z = lax.axis_index("adapter")
+    barrier = pltpu.get_barrier_semaphore()
+    for i in range(1, n):
+        pl.semaphore_signal(barrier, inc=1, **to_seq((s + i) % n))
+    for i in range(1, nz):
+        pl.semaphore_signal(barrier, inc=1, **to_adapter((z + i) % nz))
     core = s % 2
     partner = s + 1 - 2 * core
     adapt_n, rows, _ = base.shape
-    stretch, hd = keys_ref.shape
+    _, stretch, hd = k_all.shape
     tiles, wide, _ = gq_all.shape
     per = tiles // adapt_n
     factor = hd**-0.5
     pieces = stretch // chunk
-    loads = [
-        pltpu.make_async_copy(a, b, load_sem.at[i])
-        for i, (a, b) in enumerate(((hidden_hbm, hidden), (base_hbm, base), (grad_hbm, grad)))
-    ]
+    pairs = (
+        (down_hbm, down_w), (hidden_hbm, hidden), (len_hbm, len_ref), (offset_hbm, offset_ref), (up_hbm, up_w),
+        (base_hbm, base), (grad_hbm, grad), (keys_hbm, k_all.at[0]), (values_hbm, v_all.at[0]),
+    )
+    loads = [pltpu.make_async_copy(a, b, load_sem.at[i]) for i, (a, b) in enumerate(pairs)]
     for c in loads:
         c.start()
     full = (k_all, v_all)
-    own = (keys_ref, values_ref)
+    own = (keys_hbm, values_hbm)
 
     def copy(i, src, slot, which, target):
         return remote(src, full[i].at[slot], send_sem.at[which, i], recv_sem.at[slot, i], to_seq(target))
@@ -75,8 +82,24 @@
                 full[i].at[slot], full[i].at[slot], send_sem.at[0, i], recv_sem.at[slot, i], to_seq(partner)
             ).wait_recv()
 
-    z = lax.axis_index("adapter")
     has_three_in = (core == 1) & (s + 3 < n)
+    pl.semaphore_wait(barrier, n - 1 + nz - 1)
+
+    has_two_on = s + 2 < n
+    has_three_on = (core == 1) & (s + 3 < n)
+    for i in range(2):
+
+        @pl.when(has_two_on)
+        def _():
+            two_on[i].start()
+
+        @pl.when(has_three_on)
+        def _():
+            three_on[i].start()
+
+        @pl.when(core == 0)
+        def _():
+            next_on[i].start()
 
     @pl.when(s + 2 >= n)
     def _():
@@ -90,31 +113,6 @@
     def _():
         pair_b[...] = jnp.zeros_like(pair_b)
 
-    barrier = pltpu.get_barrier_semaphore()
-    for i in range(1, n):
-        pl.semaphore_signal(barrier, inc=1, **to_seq((s + i) % n))
-    for i in range(1, nz):
-        pl.semaphore_signal(barrier, inc=1, **to_adapter((z + i) % nz))
-    pl.semaphore_wait(barrier, n - 1 + nz - 1)
-
-    has_two_on = s + 2 < n
-    has_three_on = (core == 1) & (s + 3 < n)
-    for i in range(2):
-
-        @pl.when(has_two_on)
-        def _():
-            two_on[i].start()
-
-        @pl.when(has_three_on)
-        def _():
-            three_on[i].start()
-
-        @pl.when(core == 0)
-        def _():
-            next_on[i].start()
-
-    k_all[0] = keys_ref[...]
-    v_all[0] = values_ref[...]
     for slot in (1, 2, 3):
 
         @pl.when(s < slot)
@@ -138,6 +136,8 @@
             t, at_row = a * per + h // heads, (h % heads) * rows
             gq_all[t, at_row : at_row + rows, :hd] = g[:, h * hd : (h + 1) * hd]
             gq_all[t, at_row : at_row + rows, hd:] = query[:, h * hd : (h + 1) * hd]
+            g_turned[t, :, at_row : at_row + rows] = g[:, h * hd : (h + 1) * hd].T
+            q_turned[t, :, at_row : at_row + rows] = query[:, h * hd : (h + 1) * hd].T
 
     def hand(i):
         @pl.when(s >= 2)
@@ -163,14 +163,14 @@
         kt[:, spots[d] * stretch : (spots[d] + 1) * stretch] = k_all[d].T
 
     def product(source, d, piece, other):
-        return dot(source[d, at(piece), :], other, ((1,), (1,)))
+        return dot(source[d, at(piece), :], other, ((1,), (0,)))
 
     far_bias = jnp.where(s >= 3, 0.0, masked_score)
 
     @pl.loop(0, tiles)
     def _(t):
-        q = gq_all[t, :, hd:]
-        g = gq_all[t, :, :hd]
+        q = q_turned[t]
+        g = g_turned[t]
         for piece in range(pieces):
             s_ref[t, at(piece), :] = product(k_all, 0, piece, q) * factor
             dp_ref[t, at(piece), :] = product(v_all, 0, piece, g)
@@ -178,7 +178,7 @@
     def scores_of(d):
         @pl.loop(0, tiles)
         def _(t):
-            q = gq_all[t, :, hd:]
+            q = q_turned[t]
             peak = jnp.full((1, wide), masked_score, jnp.float32)
             for piece in range(pieces):
                 score = product(k_all, d or 3, piece, q) * factor
@@ -192,7 +192,7 @@
     def raise_of(d):
         @pl.loop(0, tiles)
         def _(t):
-            g = gq_all[t, :, :hd]
+            g = g_turned[t]
             peak = peaks[d, t]
             total = jnp.zeros((1, wide), jnp.float32)
             inner = jnp.zeros((1, wide), jnp.float32)
@@ -455,9 +455,21 @@
         c.wait_recv()
         mine = mine + down_in[i].astype(jnp.float32)
     down_out[...] = mine
+    results = [
+        pltpu.make_async_copy(down_out, down_result, out_sem.at[0]),
+        pltpu.make_async_copy(up_out, up_result, out_sem.at[1]),
+        pltpu.make_async_copy(prompt_out.at[0], prompt_result.at[0], out_sem.at[2]),
+        pltpu.make_async_copy(prompt_out.at[1], prompt_result.at[1], out_sem.at[3]),
+    ]
+    results[0].start()
     prompt_sum(1)
+    results[3].start()
     prompt_sum(0)
+    results[2].start()
     up_back.wait_recv()
+    results[1].start()
+    for c in results:
+        c.wait()
     for c in downs + ups + spread[0] + spread[1] + zero_to_one + [up_swap, down_swap, up_back]:
         c.wait_send()
     for i in range(2):
@@ -501,11 +513,10 @@
     heads = 4
     wide = heads * row_n
     tiles = adapt_n * feature_n // (hd * heads)
-    chunk = 256 if stretch % 256 == 0 else stretch
+    chunk = stretch
     quarter = stretch // nz
     up_shape = (2, ranks, feature_n // 2)
     down_shape = (n // 2, ranks, model // n)
-    spec = pl.BlockSpec(memory_space=VMEM)
     anywhere = pl.BlockSpec(memory_space=pl.ANY)
     dma = pltpu.SemaphoreType.DMA
     bf16 = jnp.bfloat16
@@ -519,9 +530,16 @@
             jax.ShapeDtypeStruct(up_shape, f32),
             jax.ShapeDtypeStruct((2, quarter, hd), f32),
         ),
-        in_specs=[pl.BlockSpec(memory_space=pltpu.SMEM)] + [anywhere] * 3 + [spec] * 5,
-        out_specs=(spec, spec, spec),
+        in_specs=[anywhere] * 9,
+        out_specs=(anywhere,) * 3,
         scratch_shapes=[
+            pltpu.SMEM(lengths.shape, jnp.int32),
+            VMEM(down_w.shape, bf16),
+            VMEM(up_w.shape, bf16),
+            VMEM((adapt_n, 1, row_n), jnp.int32),
+            VMEM((ranks, model // n), f32),
+            VMEM(up_shape, f32),
+            VMEM((2, quarter, hd), f32),
             VMEM((adapt_n, row_n, rank), bf16),
             VMEM((tiles, wide, hd), bf16),
             VMEM((4, 2, stretch, hd), bf16),
@@ -529,6 +547,8 @@
             VMEM(base.shape, bf16),
             VMEM(grad.shape, bf16),
             VMEM((tiles, wide, 2 * hd), bf16),
+            VMEM((tiles, hd, wide), bf16),
+            VMEM((tiles, hd, wide), bf16),
             VMEM((4, stretch, hd), bf16),
             VMEM((4, stretch, hd), bf16),
             VMEM((hd, 4 * stretch), bf16),
@@ -539,7 +559,7 @@
             VMEM((tiles, 1, wide), jnp.int32),
             VMEM((stretch, hd), f32),
             VMEM((tiles, hd, wide), f32),
-            dma((3,)), dma((3, 2)), dma((4, 2)),
+            dma((9,)), dma((4,)), dma((3, 2)), dma((4, 2)),
             VMEM((2,) + down_shape, bf16),
             VMEM(up_shape, bf16),
             block, block, block, block, block, block,

time: 53.7 us -> 52.2 us (0.972)
  Pallas kernels: 52.9 us -> 51.4 us
    pallas_call x1, Pallas kernels: 51 us -> 49.5 us  [gradients(): pl.pallas_call(functools.partial(attend_kernel, n, nz, heads, chunk), out...]
where the time goes in v4:
time: 52.2 us; the launch traced here: 52 us
  Pallas kernels  51.4 us (98%)
  between operations  0.64 us (1%)
    pallas_call x1, Pallas kernels, gradients(): pl.pallas_call(functools.partial(attend_kernel, n, nz, heads, chunk), out...  49.5 us
    pallas_call x1, Pallas kernels, finish(): pl.pallas_call(finish_kernel, out_shape=(jax.ShapeDtypeStruct((adapt_n, r...  1.87 us

profile of v4, /device:TPU:0, one launch (start us, length us, event | category | flops | bytes accessed | tf_op | source)
XLA Modules:
  0.0 52.0 jit_solution(2683980805357908895)
XLA Ops:
  0.6 49.5 %gradients.1 = (f32[32,1024]{1,0:T(8,128)}, f32[2,32,512]{2,1,0:T(8,128)}, f32[2,192,128]{2,1,0:T(8,128)}) custom-call(s32[2]{0:T(128)} %len_hbm.1, bf16[2,128,8192]{2,1,0:T(8,128)(2,1)} %hidden_hbm.1, bf16[2,128,1024]{2,1,0:T(8,128)(2,1)} %base_hbm.1, bf16[2,128,1024]{2,1,0:T(8,128)(2,1)} %grad_hbm.1, bf16[2,16,8192]{2,1,0:T(8,128)(2,1)} %down_hbm.1, ...), custom_call_target="tpu_custom_call" | custom-call | tf_op jit(solution)/shard_map/gradients/pallas_call | solution.py:526
  50.2 1.9 %finish.1 = (f32[2,16,1024]{2,1,0:T(8,128)}, f32[2,16,1024]{2,1,0:T(8,128)}, f32[192,128]{1,0:T(8,128)}, f32[192,128]{1,0:T(8,128)}) custom-call(f32[32,1024]{1,0:T(8,128)} %get-tuple-element.7.down_hbm, f32[2,32,512]{2,1,0:T(8,128)} %get-tuple-element.8.up_hbm, f32[2,192,128]{2,1,0:T(8,128)} %get-tuple-element.9.prompt_hbm), custom_call_target="tpu_custom_call" | custom-call | tf_op jit(solution)/shard_map/finish/pallas_call | solution.py:602

commit v5 on v4

--- a/solution.py
+++ b/solution.py
@@ -8,6 +8,7 @@
 from jax.sharding import PartitionSpec as P
 
 adapter_scale = 2.0
+at_once = 2
 masked_score = -1e30
 MESH = pl.DeviceIdType.MESH
 VMEM = pltpu.VMEM
@@ -153,6 +154,22 @@
     def at(piece):
         return slice(piece * chunk, (piece + 1) * chunk)
 
+    def each(first, last):
+        step = at_once if (last - first) % at_once == 0 else 1
+
+        def run(body):
+            if last - first == step:
+                for j in range(first, last):
+                    body(j)
+                return
+
+            @pl.loop(first, last, step=step)
+            def _(t):
+                for j in range(step):
+                    body(t + j)
+
+        return run
+
     def before(piece, place):
         pos = piece * chunk + lax.broadcasted_iota(jnp.int32, (chunk, wide), 0)
         return pos <= place
@@ -167,7 +184,7 @@
 
     far_bias = jnp.where(s >= 3, 0.0, masked_score)
 
-    @pl.loop(0, tiles)
+    @each(0, tiles)
     def _(t):
         q = q_turned[t]
         g = g_turned[t]
@@ -176,7 +193,7 @@
             dp_ref[t, at(piece), :] = product(v_all, 0, piece, g)
 
     def scores_of(d):
-        @pl.loop(0, tiles)
+        @each(0, tiles)
         def _(t):
             q = q_turned[t]
             peak = jnp.full((1, wide), masked_score, jnp.float32)
@@ -190,7 +207,7 @@
             peaks[d, t] = peak
 
     def raise_of(d):
-        @pl.loop(0, tiles)
+        @each(0, tiles)
         def _(t):
             g = g_turned[t]
             peak = peaks[d, t]
@@ -228,7 +245,7 @@
     arrived(3, 1)
     raise_of(0)
 
-    @pl.loop(0, tiles)
+    @each(0, tiles)
     def _(t):
         tops = [peaks[0, t]] + [jnp.where(s >= d, peaks[d, t], masked_score) for d in (1, 2)]
         peak = jnp.maximum(jnp.maximum(tops[0], tops[1]), tops[2])
@@ -254,7 +271,7 @@
         if first == 0:
             acc[...] = jnp.zeros_like(acc)
 
-        @pl.loop(first, last)
+        @each(first, last)
         def _(t):
             other = gq_all[t]
             share = weight[unit, t]
@@ -407,7 +424,7 @@
     third_out(0)
     gather_up(0, 0)
 
-    @pl.loop(0, tiles)
+    @each(0, tiles)
     def _(t):
         dq_ref[t] = (dq_acc[t] * factor).T.astype(jnp.bfloat16)
 

time: 52.2 us -> 50.4 us (0.966)
  Pallas kernels: 51.4 us -> 49.5 us
    pallas_call x1, Pallas kernels: 49.5 us -> 47.6 us  [gradients(): pl.pallas_call(functools.partial(attend_kernel, n, nz, heads, chunk), out...]
where the time goes in v5:
time: 50.4 us; the launch traced here: 50.3 us
  Pallas kernels  49.5 us (98%)
  between operations  0.8 us (2%)
    pallas_call x1, Pallas kernels, gradients(): pl.pallas_call(functools.partial(attend_kernel, n, nz, heads, chunk), out...  47.6 us
    pallas_call x1, Pallas kernels, finish(): pl.pallas_call(finish_kernel, out_shape=(jax.ShapeDtypeStruct((adapt_n, r...  1.87 us

profile of v5, /device:TPU:0, one launch (start us, length us, event | category | flops | bytes accessed | tf_op | source)
XLA Modules:
  0.0 50.3 jit_solution(10846405466889968424)
XLA Ops:
  0.6 47.6 %gradients.1 = (f32[32,1024]{1,0:T(8,128)}, f32[2,32,512]{2,1,0:T(8,128)}, f32[2,192,128]{2,1,0:T(8,128)}) custom-call(s32[2]{0:T(128)} %len_hbm.1, bf16[2,128,8192]{2,1,0:T(8,128)(2,1)} %hidden_hbm.1, bf16[2,128,1024]{2,1,0:T(8,128)(2,1)} %base_hbm.1, bf16[2,128,1024]{2,1,0:T(8,128)(2,1)} %grad_hbm.1, bf16[2,16,8192]{2,1,0:T(8,128)(2,1)} %down_hbm.1, ...), custom_call_target="tpu_custom_call" | custom-call | tf_op jit(solution)/shard_map/gradients/pallas_call | solution.py:543
  48.2 1.9 %finish.1 = (f32[2,16,1024]{2,1,0:T(8,128)}, f32[2,16,1024]{2,1,0:T(8,128)}, f32[192,128]{1,0:T(8,128)}, f32[192,128]{1,0:T(8,128)}) custom-call(f32[32,1024]{1,0:T(8,128)} %get-tuple-element.7.down_hbm, f32[2,32,512]{2,1,0:T(8,128)} %get-tuple-element.8.up_hbm, f32[2,192,128]{2,1,0:T(8,128)} %get-tuple-element.9.prompt_hbm), custom_call_target="tpu_custom_call" | custom-call | tf_op jit(solution)/shard_map/finish/pallas_call | solution.py:619

commit v6 on v5

--- a/solution.py
+++ b/solution.py
@@ -278,9 +278,14 @@
             lows = []
             for piece in range(pieces):
                 spot = rows_of(unit, piece)
-                value = s_ref[t, spot, :] * share
-                if i == 0:
-                    value = value * (dp_ref[t, spot, :] - delta[t])
+                if i == 0 and static and block == 0:
+                    value = dp_ref[t, spot, :]
+                else:
+                    value = s_ref[t, spot, :] * share
+                    if i == 0:
+                        value = value * (dp_ref[t, spot, :] - delta[t])
+                    if i == 0 and static:
+                        dp_ref[t, spot, :] = value
                 if static:
                     near = before(piece, place_ref[t])
                     value = jnp.where(near, 0.0, value) if block else jnp.where(near, value, 0.0)
@@ -453,13 +458,13 @@
     up_all[chip] = (up[core].astype(jnp.float32) + up_pair[...].astype(jnp.float32)).astype(jnp.bfloat16)
     for c in ups:
         c.start()
+    owner(0)
     down_swap.wait_recv()
     for j in range(chips):
         both = down[core, j].astype(jnp.float32) + down_pair[j].astype(jnp.float32)
         down_chip[j] = both.astype(jnp.bfloat16)
     for c in downs:
         c.start()
-    owner(0)
     for c in ups:
         c.wait_recv()
     mine = up_all[0].astype(jnp.float32)

time: 50.4 us -> 49.9 us (0.990)
  Pallas kernels: 49.5 us -> 48.9 us
    pallas_call x1, Pallas kernels: 47.6 us -> 47 us  [gradients(): pl.pallas_call(functools.partial(attend_kernel, n, nz, heads, chunk), out...]
where the time goes in v6:
time: 49.9 us; the launch traced here: 49.7 us
  Pallas kernels  48.9 us (98%)
  between operations  0.8 us (2%)
    pallas_call x1, Pallas kernels, gradients(): pl.pallas_call(functools.partial(attend_kernel, n, nz, heads, chunk), out...  47 us
    pallas_call x1, Pallas kernels, finish(): pl.pallas_call(finish_kernel, out_shape=(jax.ShapeDtypeStruct((adapt_n, r...  1.87 us

profile of v6, /device:TPU:0, one launch (start us, length us, event | category | flops | bytes accessed | tf_op | source)
XLA Modules:
  0.0 49.7 jit_solution(5555005967996586746)
XLA Ops:
  0.6 47.0 %gradients.1 = (f32[32,1024]{1,0:T(8,128)}, f32[2,32,512]{2,1,0:T(8,128)}, f32[2,192,128]{2,1,0:T(8,128)}) custom-call(s32[2]{0:T(128)} %len_hbm.1, bf16[2,128,8192]{2,1,0:T(8,128)(2,1)} %hidden_hbm.1, bf16[2,128,1024]{2,1,0:T(8,128)(2,1)} %base_hbm.1, bf16[2,128,1024]{2,1,0:T(8,128)(2,1)} %grad_hbm.1, bf16[2,16,8192]{2,1,0:T(8,128)(2,1)} %down_hbm.1, ...), custom_call_target="tpu_custom_call" | custom-call | tf_op jit(solution)/shard_map/gradients/pallas_call | solution.py:548
  47.7 1.9 %finish.1 = (f32[2,16,1024]{2,1,0:T(8,128)}, f32[2,16,1024]{2,1,0:T(8,128)}, f32[192,128]{1,0:T(8,128)}, f32[192,128]{1,0:T(8,128)}) custom-call(f32[32,1024]{1,0:T(8,128)} %get-tuple-element.7.down_hbm, f32[2,32,512]{2,1,0:T(8,128)} %get-tuple-element.8.up_hbm, f32[2,192,128]{2,1,0:T(8,128)} %get-tuple-element.9.prompt_hbm), custom_call_target="tpu_custom_call" | custom-call | tf_op jit(solution)/shard_map/finish/pallas_call | solution.py:624

commit v7 on v6

--- a/solution.py
+++ b/solution.py
@@ -1,4 +1,5 @@
 import functools
+import math
 
 import jax
 import jax.numpy as jnp
@@ -56,6 +57,7 @@
     tiles, wide, _ = gq_all.shape
     per = tiles // adapt_n
     factor = hd**-0.5
+    slope = factor * math.log2(math.e)
     pieces = stretch // chunk
     pairs = (
         (down_hbm, down_w), (hidden_hbm, hidden), (len_hbm, len_ref), (offset_hbm, offset_ref), (up_hbm, up_w),
@@ -189,7 +191,7 @@
         q = q_turned[t]
         g = g_turned[t]
         for piece in range(pieces):
-            s_ref[t, at(piece), :] = product(k_all, 0, piece, q) * factor
+            s_ref[t, at(piece), :] = product(k_all, 0, piece, q)
             dp_ref[t, at(piece), :] = product(v_all, 0, piece, g)
 
     def scores_of(d):
@@ -198,7 +200,7 @@
             q = q_turned[t]
             peak = jnp.full((1, wide), masked_score, jnp.float32)
             for piece in range(pieces):
-                score = product(k_all, d or 3, piece, q) * factor
+                score = product(k_all, d or 3, piece, q)
                 if d == 0:
                     near = before(piece, place_ref[t])
                     score = jnp.where(near, s_ref[t, at(piece), :], score + far_bias)
@@ -215,7 +217,7 @@
             inner = jnp.zeros((1, wide), jnp.float32)
             for piece in range(pieces):
                 spot = at(d * pieces + piece)
-                e = jnp.exp(s_ref[t, spot, :] - peak)
+                e = jnp.exp2((s_ref[t, spot, :] - peak) * slope)
                 dp = product(v_all, d or 3, piece, g)
                 if d == 0:
                     dp = jnp.where(before(piece, place_ref[t]), dp_ref[t, spot, :], dp)
@@ -249,7 +251,7 @@
     def _(t):
         tops = [peaks[0, t]] + [jnp.where(s >= d, peaks[d, t], masked_score) for d in (1, 2)]
         peak = jnp.maximum(jnp.maximum(tops[0], tops[1]), tops[2])
-        shares = [jnp.exp(top - peak) for top in tops]
+        shares = [jnp.exp2((top - peak) * slope) for top in tops]
         total = jnp.zeros((1, wide), jnp.float32)
         inner = jnp.zeros((1, wide), jnp.float32)
         for d, share in enumerate(shares):

time: 49.9 us -> 49.7 us (level)
  no operation moved by 1% of the time
where the time goes in v7:
time: 49.7 us; the launch traced here: 49.5 us
  Pallas kernels  48.7 us (98%)
  between operations  0.8 us (2%)
    pallas_call x1, Pallas kernels, gradients(): pl.pallas_call(functools.partial(attend_kernel, n, nz, heads, chunk), out...  46.8 us
    pallas_call x1, Pallas kernels, finish(): pl.pallas_call(finish_kernel, out_shape=(jax.ShapeDtypeStruct((adapt_n, r...  1.87 us

profile of v7, /device:TPU:0, one launch (start us, length us, event | category | flops | bytes accessed | tf_op | source)
XLA Modules:
  0.0 49.5 jit_solution(4516644494253337186)
XLA Ops:
  0.6 46.8 %gradients.1 = (f32[32,1024]{1,0:T(8,128)}, f32[2,32,512]{2,1,0:T(8,128)}, f32[2,192,128]{2,1,0:T(8,128)}) custom-call(s32[2]{0:T(128)} %len_hbm.1, bf16[2,128,8192]{2,1,0:T(8,128)(2,1)} %hidden_hbm.1, bf16[2,128,1024]{2,1,0:T(8,128)(2,1)} %base_hbm.1, bf16[2,128,1024]{2,1,0:T(8,128)(2,1)} %grad_hbm.1, bf16[2,16,8192]{2,1,0:T(8,128)(2,1)} %down_hbm.1, ...), custom_call_target="tpu_custom_call" | custom-call | tf_op jit(solution)/shard_map/gradients/pallas_call | solution.py:550
  47.5 1.9 %finish.1 = (f32[2,16,1024]{2,1,0:T(8,128)}, f32[2,16,1024]{2,1,0:T(8,128)}, f32[192,128]{1,0:T(8,128)}, f32[192,128]{1,0:T(8,128)}) custom-call(f32[32,1024]{1,0:T(8,128)} %get-tuple-element.7.down_hbm, f32[2,32,512]{2,1,0:T(8,128)} %get-tuple-element.8.up_hbm, f32[2,192,128]{2,1,0:T(8,128)} %get-tuple-element.9.prompt_hbm), custom_call_target="tpu_custom_call" | custom-call | tf_op jit(solution)/shard_map/finish/pallas_call | solution.py:626

commit v8 on v7

--- a/solution.py
+++ b/solution.py
@@ -156,8 +156,8 @@
     def at(piece):
         return slice(piece * chunk, (piece + 1) * chunk)
 
-    def each(first, last):
-        step = at_once if (last - first) % at_once == 0 else 1
+    def each(first, last, most=at_once):
+        step = math.gcd(most, last - first)
 
         def run(body):
             if last - first == step:
@@ -186,7 +186,7 @@
 
     far_bias = jnp.where(s >= 3, 0.0, masked_score)
 
-    @each(0, tiles)
+    @each(0, tiles, 4)
     def _(t):
         q = q_turned[t]
         g = g_turned[t]
@@ -195,7 +195,7 @@
             dp_ref[t, at(piece), :] = product(v_all, 0, piece, g)
 
     def scores_of(d):
-        @each(0, tiles)
+        @each(0, tiles, 4)
         def _(t):
             q = q_turned[t]
             peak = jnp.full((1, wide), masked_score, jnp.float32)
@@ -209,7 +209,7 @@
             peaks[d, t] = peak
 
     def raise_of(d):
-        @each(0, tiles)
+        @each(0, tiles, 4)
         def _(t):
             g = g_turned[t]
             peak = peaks[d, t]
@@ -247,7 +247,7 @@
     arrived(3, 1)
     raise_of(0)
 
-    @each(0, tiles)
+    @each(0, tiles, 4)
     def _(t):
         tops = [peaks[0, t]] + [jnp.where(s >= d, peaks[d, t], masked_score) for d in (1, 2)]
         peak = jnp.maximum(jnp.maximum(tops[0], tops[1]), tops[2])
@@ -462,10 +462,10 @@
         c.start()
     owner(0)
     down_swap.wait_recv()
-    for j in range(chips):
-        both = down[core, j].astype(jnp.float32) + down_pair[j].astype(jnp.float32)
-        down_chip[j] = both.astype(jnp.bfloat16)
-    for c in downs:
+    for i, c in enumerate(downs):
+        peer = (chip + i + 1) % chips
+        both = down[core, peer].astype(jnp.float32) + down_pair[peer].astype(jnp.float32)
+        down_chip[peer] = both.astype(jnp.bfloat16)
         c.start()
     for c in ups:
         c.wait_recv()

time: 49.7 us -> 49.3 us (level)
  no operation moved by 1% of the time
where the time goes in v8:
time: 49.3 us; the launch traced here: 49.2 us
  Pallas kernels  48.4 us (98%)
  between operations  0.8 us (2%)
    pallas_call x1, Pallas kernels, gradients(): pl.pallas_call(functools.partial(attend_kernel, n, nz, heads, chunk), out...  46.5 us
    pallas_call x1, Pallas kernels, finish(): pl.pallas_call(finish_kernel, out_shape=(jax.ShapeDtypeStruct((adapt_n, r...  1.87 us

profile of v8, /device:TPU:0, one launch (start us, length us, event | category | flops | bytes accessed | tf_op | source)
XLA Modules:
  0.0 49.2 jit_solution(18063263819053434958)
XLA Ops:
  0.6 46.5 %gradients.1 = (f32[32,1024]{1,0:T(8,128)}, f32[2,32,512]{2,1,0:T(8,128)}, f32[2,192,128]{2,1,0:T(8,128)}) custom-call(s32[2]{0:T(128)} %len_hbm.1, bf16[2,128,8192]{2,1,0:T(8,128)(2,1)} %hidden_hbm.1, bf16[2,128,1024]{2,1,0:T(8,128)(2,1)} %base_hbm.1, bf16[2,128,1024]{2,1,0:T(8,128)(2,1)} %grad_hbm.1, bf16[2,16,8192]{2,1,0:T(8,128)(2,1)} %down_hbm.1, ...), custom_call_target="tpu_custom_call" | custom-call | tf_op jit(solution)/shard_map/gradients/pallas_call | solution.py:550
  47.2 1.9 %finish.1 = (f32[2,16,1024]{2,1,0:T(8,128)}, f32[2,16,1024]{2,1,0:T(8,128)}, f32[192,128]{1,0:T(8,128)}, f32[192,128]{1,0:T(8,128)}) custom-call(f32[32,1024]{1,0:T(8,128)} %get-tuple-element.7.down_hbm, f32[2,32,512]{2,1,0:T(8,128)} %get-tuple-element.8.up_hbm, f32[2,192,128]{2,1,0:T(8,128)} %get-tuple-element.9.prompt_hbm), custom_call_target="tpu_custom_call" | custom-call | tf_op jit(solution)/shard_map/finish/pallas_call | solution.py:626
